TPU v7x, 256 devices: a whole 4x4x8 slice. The times are simulated.
256 devices in a mesh: root: 8 (over z), virt: 16 (over x, y), occ: 2 (over core).
Axes of the slice: x: 4, y: 4, z: 8, core: 2. Of those that a mesh axis runs over, the one named last changes fastest.
Arguments:
- trial_singles: bfloat16 [16, 96], P('root'), may hold values from -6 to 6
- trial_doubles: bfloat16 [16, 480, 9216], P('root', 'virt', 'occ'), may hold values from -6 to 6
- occ_fock: bfloat16 [96, 96], replicated, may hold values from -0.625 to 0.625
- virt_fock: bfloat16 [480, 480], replicated, may hold values from -0.25 to 0.25
- w_ovoo: bfloat16 [96, 480, 9216], P('occ', 'virt', 'root'), may hold values from -0.625 to 0.625
- w_ooov: bfloat16 [96, 480, 9216], P('occ', 'virt', 'root'), may hold values from -0.0029296875 to 0.0029296875
- converged: int32 [16], replicated, may hold values from 0 to 1, as said below
Outputs:
- sigma_doubles: bfloat16 [16, 480, 9216], P('root', 'virt', 'occ')
- sigma_singles: float32 [16, 96], P('root')
- subspace: float32 [16, 16], P('root')
Inputs may be any that keep to these rules, and one draw needn't show every extreme that they name: `converged`: exactly 8 roots are active (0). In every draw at least one aligned block of 2 roots has all its roots active; other blocks may have none.
All inputs are finite; a program needn't handle non-finite values.
Results may differ from a plain program's by a relative error of at most 0.0044.
Values may be sent and summed in bfloat16 or wider, within the bound.
No kernel may reach another device: no remote copies, remote signals or barrier semaphores. Data moves between devices by JAX's collectives and lax.ppermute only.
A program may use at most 256 MiB of HBM per device.

v0:
```python
import functools
import math
import jax
import jax.numpy as jnp
from jax import lax
from jax.sharding import Mesh
from jax.sharding import PartitionSpec as P

ROOT_VIRT_OCC = ("root", "virt_0", "virt_1", "occ")
VIRT = ("virt_0", "virt_1")


def laid_out(parts, dim):
    parts = jnp.moveaxis(parts, 0, dim)
    shape = parts.shape
    return parts.reshape(*shape[:dim], shape[dim] * shape[dim + 1], *shape[dim + 2 :])


def from_everyone(array, axis):
    copies = jnp.broadcast_to(array, (lax.axis_size(axis), *array.shape))
    return lax.all_to_all(copies, axis, split_axis=0, concat_axis=0, tiled=True)


def gather_directly(array, axis, dim):
    return laid_out(from_everyone(array, axis), dim)


def by_axis(array, axes):
    return functools.reduce(lax.psum, axes, array)


def in_blocks(array, dim, devices):
    before, after = (array.shape[:dim], array.shape[dim + 1 :])
    return jnp.moveaxis(array.reshape(*before, devices, -1, *after), dim, 0)


def sum_at_owner(array, axis, dim):
    parts = in_blocks(array, dim, lax.axis_size(axis))
    arrived = lax.all_to_all(parts, axis, split_axis=0, concat_axis=0, tiled=True)
    return arrived.astype(jnp.float32).sum(axis=0)


def in_one_piece(arrays, axis, split_dim, concat_dim, along):
    ends, at = ([], 0)
    for a in arrays[:-1]:
        at += a.shape[along]
        ends.append(at)
    both = jnp.concatenate(arrays, axis=along)
    return tuple(
        jnp.split(
            lax.all_to_all(both, axis, split_axis=split_dim, concat_axis=concat_dim, tiled=True),
            ends,
            axis=along,
        )
    )


def flat_pairs(left, right):
    return lax.dot_general(
        left.reshape(left.shape[0], -1),
        right.reshape(right.shape[0], -1),
        (((1,), (1,)), ((), ())),
        preferred_element_type=jnp.float32,
    )


def local(trial_singles, trial_doubles, occ_fock, virt_fock, w_ovoo, w_ooov, converged):
    local_roots, virt_local, pair_local = trial_doubles.shape
    occ_count = occ_fock.shape[0]
    virt_count = virt_fock.shape[0]
    root_count = converged.shape[0]
    root_groups = lax.axis_size("root")
    occ_groups = lax.axis_size("occ")
    root_index = lax.axis_index("root")
    occ_index = lax.axis_index("occ")
    occ_half = occ_count // occ_groups
    block_pairs = occ_count * occ_count // root_groups
    own_start = occ_index * occ_half
    active = (1 - converged).astype(jnp.float32)
    own_active = lax.dynamic_slice_in_dim(active, root_index * local_roots, local_roots)
    singles_all = gather_directly(trial_singles, "root", 0)
    gathered = gather_directly(trial_doubles, "occ", 2)
    fock_cols = lax.dynamic_slice_in_dim(occ_fock, own_start, occ_half, 1)
    batch_rows = local_roots * virt_local
    stacked = gathered.reshape(batch_rows, occ_count, occ_count)
    first_term = jnp.einsum(
        "ki,bkj->bij", fock_cols, stacked, preferred_element_type=jnp.float32
    ).reshape(local_roots, virt_local, pair_local)
    own_rows = trial_doubles.reshape(batch_rows, occ_half, occ_count)
    second_term = jnp.einsum(
        "bik,kj->bij", own_rows, occ_fock, preferred_element_type=jnp.float32
    ).reshape(local_roots, virt_local, pair_local)
    doubles_block = lax.all_to_all(gathered, "root", split_axis=2, concat_axis=0, tiled=True)
    partial_coupling = flat_pairs(doubles_block, w_ooov)
    coupling_part = lax.dynamic_update_slice(
        jnp.zeros((root_count, occ_count), jnp.float32), partial_coupling, (jnp.int32(0), own_start)
    )
    coupling = by_axis(coupling_part, ROOT_VIRT_OCC)
    singles_fock = jnp.dot(singles_all, occ_fock, preferred_element_type=jnp.float32)
    singles_every = active[:, None] * (-singles_fock - 0.5 * coupling)
    sigma_singles = lax.dynamic_slice_in_dim(singles_every, root_index * local_roots, local_roots)
    singles_cols = lax.dynamic_slice_in_dim(singles_all, own_start, occ_half, 1)
    outer_part = (
        -jnp.dot(singles_cols, w_ovoo.reshape(occ_half, -1), preferred_element_type=jnp.float32)
    ).reshape(root_count, virt_local, block_pairs)
    product = jnp.einsum(
        "ac,ncp->nap",
        virt_fock,
        lax.all_to_all(trial_doubles, VIRT, split_axis=2, concat_axis=1, tiled=True),
        preferred_element_type=jnp.float32,
    ).astype(jnp.bfloat16)
    vv_term = lax.all_to_all(product, VIRT, split_axis=1, concat_axis=2, tiled=True)
    vv_value = vv_term.astype(jnp.float32)
    outer_own = lax.all_to_all(
        outer_part.astype(jnp.bfloat16), "root", split_axis=0, concat_axis=2, tiled=True
    ).astype(outer_part.dtype)
    outer_half = sum_at_owner(outer_own.astype(jnp.bfloat16), "occ", 2)
    summed = vv_value + outer_half - first_term - second_term
    sigma_doubles = (own_active[:, None, None] * summed).astype(jnp.bfloat16)
    trial_piece, sigma_piece = in_one_piece((trial_doubles, sigma_doubles), "root", 2, 0, 1)
    doubles_part = by_axis(flat_pairs(trial_piece, sigma_piece), ROOT_VIRT_OCC)
    singles_part = jnp.dot(
        singles_all.astype(jnp.float32), singles_every.T, precision=lax.Precision.HIGHEST
    )
    whole_matrix = doubles_part / math.sqrt(
        occ_count * occ_count * virt_count
    ) + singles_part / math.sqrt(occ_count)
    subspace = lax.dynamic_slice_in_dim(whole_matrix, root_index * local_roots, local_roots, 0)
    return (sigma_doubles, sigma_singles, subspace)


def solution(mesh):
    torus = Mesh(
        mesh.devices.reshape(mesh.shape["root"], 4, 4, mesh.shape["occ"]),
        ("root", "virt_0", "virt_1", "occ"),
    )
    return jax.shard_map(
        local,
        mesh=torus,
        in_specs=(
            P("root", None),
            P("root", VIRT, "occ"),
            P(),
            P(),
            P("occ", VIRT, "root"),
            P("occ", VIRT, "root"),
            P(),
        ),
        out_specs=(P("root", VIRT, "occ"), P("root", None), P("root", None)),
        check_vma=False,
    )
```

profile of v0, /device:TPU:1, one launch (start us, length us, event | category | flops | bytes accessed | tf_op | source)
XLA Modules:
  0.0 282.3 jit_solution(16731073412498609034)
XLA Ops:
  0.6 5.3 %copy.72 = bf16[2,30,4608]{1,0,2:T(2,128)(2,1)S(1)} copy(bf16[2,30,4608]{2,0,1:T(2,128)(2,1)} %param.8) | data formatting | bytes 1105920 | tf_op args[1]
  5.9 4.5 %reshape.61 = bf16[16,2,8640]{2,1,0:T(2,128)(2,1)S(1)} reshape(bf16[4608,2,30]{2,1,0:T(2,128)(2,1)S(1)} %bitcast.77) | data formatting | bytes 1105920
  10.5 18.6 %all_to_all.90 = bf16[16,2,8640]{2,1,0:T(2,128)(2,1)S(1)} all-to-all(bf16[16,2,8640]{2,1,0:T(2,128)(2,1)S(1)} %reshape.61), channel_id=1, replica_groups=mesh['root'=8,'virt_0'=4,'virt_1'=4,'occ'=2] {'virt_0','virt_1'}, dimensions={0} | all-to-all | bytes 1105920 | tf_op jit(solution)/shard_map/all_to_all | solution.py:109
  30.6 5.5 %all-to-all-start.5 = ((bf16[2,2,30,4608]{3,1,2,0:T(2,128)(2,1)}), bf16[2,2,30,4608]{3,1,2,0:T(2,128)(2,1)S(1)}, u32[]{:S(2)}, u32[]{:S(2)}) async-start(bf16[2,2,30,4608]{3,1,2,0:T(2,128)(2,1)} %broadcast_in_dim.12), calls=%async_computation.5 | async-start | bytes 2211840 | tf_op jit(solution)/shard_map/all_to_all | solution.py:21
  36.1 7.4 %reshape.62 = bf16[4608,2,30]{2,1,0:T(2,128)(2,1)} reshape(bf16[16,2,8640]{2,1,0:T(2,128)(2,1)S(1)} %all_to_all.90) | data formatting | bytes 1105920
  43.5 5.5 %copy.73 = bf16[2,30,16,288]{3,0,1,2:T(2,128)(2,1)S(1)} copy(bf16[2,30,16,288]{1,0,3,2:T(2,128)(2,1)} %bitcast.74) | data formatting | bytes 1105920 | tf_op jit(solution)/shard_map/all_to_all | solution.py:109
  49.6 8.2 %all-to-all-start.2 = ((bf16[8,2,96]{2,1,0:T(2,128)(2,1)}), bf16[8,2,96]{2,1,0:T(2,128)(2,1)S(1)}, u32[]{:S(2)}, u32[]{:S(2)}) async-start(bf16[8,2,96]{2,1,0:T(2,128)(2,1)} %broadcast_in_dim.11), calls=%async_computation.2 | async-start | bytes 8192 | tf_op jit(solution)/shard_map/all_to_all | solution.py:21
  60.3 3.9 %all-to-all-done.2 = bf16[8,2,96]{2,1,0:T(2,128)(2,1)S(1)} async-done(((bf16[8,2,96]{2,1,0:T(2,128)(2,1)}), bf16[8,2,96]{2,1,0:T(2,128)(2,1)S(1)}, u32[]{:S(2)}, u32[]{:S(2)}) %all-to-all-start.2) | async-done | bytes 3104 | tf_op jit(solution)/shard_map/all_to_all | solution.py:21
  64.2 4.3 %all-to-all-start.1 = ((bf16[2,480,288]{2,0,1:T(2,128)(2,1)}), bf16[2,480,288]{2,0,1:T(2,128)(2,1)}, u32[]{:S(2)}, u32[]{:S(2)}) async-start(bf16[2,480,288]{2,0,1:T(2,128)(2,1)} %copy.75), calls=%async_computation.1 | async-start | bytes 1474560 | tf_op jit(solution)/shard_map/all_to_all | solution.py:112
  68.5 3.9 %copy.108 = bf16[30,6,8,1152]{3,2,0,1:T(8,128)(2,1)} copy(bf16[30,6,8,1152]{3,2,1,0:T(8,128)(2,1)} %bitcast.83) | data formatting | bytes 6635520 | tf_op jit(solution)/shard_map/reshape | solution.py:104
  72.5 2.7 fusion
  76.7 4.2 %all-to-all-done.1 = bf16[2,480,288]{2,0,1:T(2,128)(2,1)} async-done(((bf16[2,480,288]{2,0,1:T(2,128)(2,1)}), bf16[2,480,288]{2,0,1:T(2,128)(2,1)}, u32[]{:S(2)}, u32[]{:S(2)}) %all-to-all-start.1) | async-done | bytes 552992 | tf_op jit(solution)/shard_map/all_to_all | solution.py:112
  81.0 4.4 %all-to-all-start.3 = ((bf16[16,30,1152]{2,1,0:T(8,128)(2,1)}), bf16[16,30,1152]{2,1,0:T(8,128)(2,1)}, u32[]{:S(2)}, u32[]{:S(2)}) async-start(bf16[16,30,1152]{2,1,0:T(8,128)(2,1)} %convert_element_type.44), calls=%async_computation.3 | async-start | bytes 2359296 | tf_op jit(solution)/shard_map/all_to_all | solution.py:114
  87.2 8.6 %copy.100 = bf16[2,30,2,4608]{1,0,3,2:T(2,128)(2,1)} copy(bf16[2,30,2,4608]{3,0,1,2:T(2,128)(2,1)S(1)} %bitcast.73) | data formatting | bytes 2211840 | tf_op jit(solution)/shard_map/reshape | solution.py:16
  102.6 10.4 %reshape.63 = bf16[8,2,34560]{2,1,0:T(2,128)(2,1)} reshape(bf16[9216,2,30]{2,1,0:T(2,128)(2,1)} %bitcast.68) | data formatting | bytes 2211840
  119.8 7.4 %all_to_all.91 = bf16[2,2,30,4608]{3,1,2,0:T(2,128)(2,1)} all-to-all(bf16[2,2,30,4608]{3,1,2,0:T(2,128)(2,1)S(1)} %copy.79), channel_id=1, replica_groups=mesh['root'=8,'virt_0'=4,'virt_1'=4,'occ'=2] {'occ'}, dimensions={0} | all-to-all | bytes 2211840 | tf_op jit(solution)/shard_map/all_to_all | solution.py:39
  127.2 6.8 %all-to-all-start.6 = ((bf16[8,2,34560]{2,1,0:T(2,128)(2,1)}), bf16[8,2,34560]{2,1,0:T(2,128)(2,1)}, u32[]{:S(2)}, u32[]{:S(2)}) async-start(bf16[8,2,34560]{2,1,0:T(2,128)(2,1)} %reshape.63), calls=%async_computation.6 | async-start | bytes 2211840 | tf_op jit(solution)/shard_map/all_to_all | solution.py:93
  133.9 3.1 %convert_reduce_fusion = f32[2,30,4608]{2,0,1:T(2,128)S(1)} fusion(bf16[2,2,30,4608]{3,1,2,0:T(2,128)(2,1)} %all_to_all.91), kind=kLoop, calls=%fused_computation.2 | loop fusion | flops 829440 | bytes 2211840 | tf_op jit(solution)/shard_map/reduce_sum | solution.py:40
  139.4 5.5 %copy.93 = bf16[2,60,4608]{1,0,2:T(2,128)(2,1)S(1)} copy(bf16[2,60,4608]{2,1,0:T(8,128)(2,1)} %pad_maximum_fusion) | data formatting | bytes 2211840 | tf_op jit(solution)/shard_map/concatenate | solution.py:48
  144.9 6.5 %reshape.65 = bf16[8,2,34560]{2,1,0:T(2,128)(2,1)} reshape(bf16[4608,2,60]{2,1,0:T(2,128)(2,1)S(1)} %bitcast.75) | data formatting | bytes 2211840
  151.4 13.1 %all-to-all-done.6 = bf16[8,2,34560]{2,1,0:T(2,128)(2,1)} async-done(((bf16[8,2,34560]{2,1,0:T(2,128)(2,1)}), bf16[8,2,34560]{2,1,0:T(2,128)(2,1)}, u32[]{:S(2)}, u32[]{:S(2)}) %all-to-all-start.6) | async-done | bytes 1105952 | tf_op jit(solution)/shard_map/all_to_all | solution.py:93
  164.5 4.3 %all-to-all-start.7 = ((bf16[8,2,34560]{2,1,0:T(2,128)(2,1)}), bf16[8,2,34560]{2,1,0:T(2,128)(2,1)}, u32[]{:S(2)}, u32[]{:S(2)}) async-start(bf16[8,2,34560]{2,1,0:T(2,128)(2,1)} %reshape.65), calls=%async_computation.7 | async-start | bytes 2211840 | tf_op jit(solution)/shard_map/all_to_all | solution.py:51
  168.8 3.9 %copy.109 = bf16[30,6,8,1152]{3,2,0,1:T(8,128)(2,1)} copy(bf16[30,6,8,1152]{3,2,1,0:T(8,128)(2,1)} %bitcast.84) | data formatting | bytes 6635520 | tf_op jit(solution)/shard_map/reshape | solution.py:61
  172.7 14.0 %reshape.64 = bf16[9216,2,30]{2,1,0:T(2,128)(2,1)} reshape(bf16[8,2,34560]{2,1,0:T(2,128)(2,1)} %all-to-all-done.6) | data formatting | bytes 2211840
  186.7 10.4 %copy.102 = bf16[2,30,8,1152]{3,1,0,2:T(8,128)(2,1)S(1)} copy(bf16[2,30,8,1152]{1,0,3,2:T(2,128)(2,1)} %bitcast.69) | data formatting | bytes 2211840 | tf_op jit(solution)/shard_map/all_to_all | solution.py:93
  197.4 2.9 %fusion.21 = f32[16,48]{1,0:T(8,128)S(1)} fusion(bf16[16,34560]{1,0:T(8,128)(2,1)S(1)} %bitcast.80, bf16[48,34560]{1,0:T(8,128)(2,1)} %bitcast.70), kind=kOutput, calls=%fused_computation.36 | convolution fusion | flops 53084160 | bytes 4426752 | tf_op jit(solution)/shard_map/dot_general | solution.py:59
  201.9 8.2 %reshape.66 = bf16[4608,2,60]{2,1,0:T(2,128)(2,1)S(1)} reshape(bf16[8,2,34560]{2,1,0:T(2,128)(2,1)} %all-to-all-done.7) | data formatting | bytes 2211840
  210.1 3.4 %copy.103 = bf16[2,60,8,576]{3,2,0,1:T(8,128)(2,1)} copy(bf16[2,60,8,576]{1,0,3,2:T(2,128)(2,1)S(1)} %bitcast.76) | data formatting | bytes 2211840 | tf_op jit(solution)/shard_map/all_to_all | solution.py:51
  217.2 22.8 %all-reduce = (f32[16,96]{1,0:T(8,128)S(1)}, f32[16,16]{1,0:T(8,128)S(1)}) all-reduce(f32[16,96]{1,0:T(8,128)S(1)} %dynamic_update_slice.3, f32[16,16]{1,0:T(8,128)S(1)} %convolution_bitcast_fusion.1), channel_id=1, replica_groups=mesh['root'=8,'virt_0'=4,'virt_1'=4,'occ'=2] {'root'}, use_global_device_ids=true, to_apply=%region_1.0 | all-reduce | flops 1792 | bytes 14336 | tf_op jit(solution)/shard_map/psum | solution.py:29
  240.1 11.4 %all-reduce.2 = (f32[16,96]{1,0:T(8,128)S(1)}, f32[16,16]{1,0:T(8,128)S(1)}) all-reduce(f32[16,96]{1,0:T(8,128)S(1)} %get-tuple-element.12, f32[16,16]{1,0:T(8,128)S(1)} %get-tuple-element.13), channel_id=1, replica_groups=mesh['root'=8,'virt_0'=4,'virt_1'=4,'occ'=2] {'virt_0'}, use_global_device_ids=true, to_apply=%region_2.0 | all-reduce | flops 1792 | bytes 14336 | tf_op jit(solution)/shard_map/psum | solution.py:29
  251.4 11.2 %all-reduce.1 = (f32[16,96]{1,0:T(8,128)S(1)}, f32[16,16]{1,0:T(8,128)S(1)}) all-reduce(f32[16,96]{1,0:T(8,128)S(1)} %get-tuple-element.16, f32[16,16]{1,0:T(8,128)S(1)} %get-tuple-element.17), channel_id=1, replica_groups=mesh['root'=8,'virt_0'=4,'virt_1'=4,'occ'=2] {'virt_1'}, use_global_device_ids=true, to_apply=%region_3.0 | all-reduce | flops 1792 | bytes 14336 | tf_op jit(solution)/shard_map/psum | solution.py:29
  262.6 18.3 %all-reduce.3 = (f32[16,96]{1,0:T(8,128)S(1)}, f32[16,16]{1,0:T(8,128)S(1)}) all-reduce(f32[16,96]{1,0:T(8,128)S(1)} %get-tuple-element.14, f32[16,16]{1,0:T(8,128)S(1)} %get-tuple-element.15), channel_id=1, replica_groups=mesh['root'=8,'virt_0'=4,'virt_1'=4,'occ'=2] {'occ'}, use_global_device_ids=true, to_apply=%region_4.0 | all-reduce | flops 1792 | bytes 14336 | tf_op jit(solution)/shard_map/psum | solution.py:29
  (59 shorter events, 30.9 us)
Async XLA Ops:
  0.6 57.1 %copy-start = (bf16[480,480]{1,0:T(8,128)(2,1)S(1)}, bf16[480,480]{1,0:T(8,128)(2,1)}, u32[]{:S(2)}) copy-start(bf16[480,480]{1,0:T(8,128)(2,1)} %param.10) | copy-start | bytes 1382404
  10.5 18.6 %copy-start.4 = (bf16[2,30,4608]{2,0,1:T(2,128)(2,1)S(1)}, bf16[2,30,4608]{2,0,1:T(2,128)(2,1)}, u32[]{:S(2)}) copy-start(bf16[2,30,4608]{2,0,1:T(2,128)(2,1)} %param.8) | copy-start | bytes 1658884
  30.6 18.4 %all-to-all-start.5 = ((bf16[2,2,30,4608]{3,1,2,0:T(2,128)(2,1)}), bf16[2,2,30,4608]{3,1,2,0:T(2,128)(2,1)S(1)}, u32[]{:S(2)}, u32[]{:S(2)}) async-start(bf16[2,2,30,4608]{3,1,2,0:T(2,128)(2,1)} %broadcast_in_dim.12), calls=%async_computation.5 | async-start | bytes 2211840 | tf_op jit(solution)/shard_map/all_to_all | solution.py:21
  43.5 5.5 %copy-start.9 = (bf16[2,96]{1,0:T(2,128)(2,1)S(1)}, bf16[2,96]{1,0:T(2,128)(2,1)}, u32[]{:S(2)}) copy-start(bf16[2,96]{1,0:T(2,128)(2,1)} %param.7) | copy-start | bytes 1156
  49.6 14.7 %all-to-all-start.2 = ((bf16[8,2,96]{2,1,0:T(2,128)(2,1)}), bf16[8,2,96]{2,1,0:T(2,128)(2,1)S(1)}, u32[]{:S(2)}, u32[]{:S(2)}) async-start(bf16[8,2,96]{2,1,0:T(2,128)(2,1)} %broadcast_in_dim.11), calls=%async_computation.2 | async-start | bytes 8192 | tf_op jit(solution)/shard_map/all_to_all | solution.py:21
  64.2 16.7 %all-to-all-start.1 = ((bf16[2,480,288]{2,0,1:T(2,128)(2,1)}), bf16[2,480,288]{2,0,1:T(2,128)(2,1)}, u32[]{:S(2)}, u32[]{:S(2)}) async-start(bf16[2,480,288]{2,0,1:T(2,128)(2,1)} %copy.75), calls=%async_computation.1 | async-start | bytes 1474560 | tf_op jit(solution)/shard_map/all_to_all | solution.py:112
  81.0 35.6 %all-to-all-start.3 = ((bf16[16,30,1152]{2,1,0:T(8,128)(2,1)}), bf16[16,30,1152]{2,1,0:T(8,128)(2,1)}, u32[]{:S(2)}, u32[]{:S(2)}) async-start(bf16[16,30,1152]{2,1,0:T(8,128)(2,1)} %convert_element_type.44), calls=%async_computation.3 | async-start | bytes 2359296 | tf_op jit(solution)/shard_map/all_to_all | solution.py:114
  95.8 1.6 copy-start.8
  97.9 1.8 copy-start.2
  102.6 10.4 %copy-start.10 = (s32[16]{0:T(128)S(1)}, s32[16]{0:T(128)}, u32[]{:S(2)}) copy-start(s32[16]{0:T(128)} %param.13) | copy-start | bytes 196
  127.2 9.9 %copy-start.6 = (f32[2,30,4608]{2,1,0:T(8,128)S(1)}, f32[2,30,4608]{2,1,0:T(8,128)}, u32[]{:S(2)}) copy-start(f32[2,30,4608]{2,1,0:T(8,128)} %reshape.50) | copy-start | bytes 3317764
  127.2 9.9 %copy-start.7 = (f32[2,30,4608]{2,1,0:T(8,128)S(1)}, f32[2,30,4608]{2,1,0:T(8,128)}, u32[]{:S(2)}) copy-start(f32[2,30,4608]{2,1,0:T(8,128)} %reshape.60) | copy-start | bytes 3317764
  127.2 37.3 %all-to-all-start.6 = ((bf16[8,2,34560]{2,1,0:T(2,128)(2,1)}), bf16[8,2,34560]{2,1,0:T(2,128)(2,1)}, u32[]{:S(2)}, u32[]{:S(2)}) async-start(bf16[8,2,34560]{2,1,0:T(2,128)(2,1)} %reshape.63), calls=%async_computation.6 | async-start | bytes 2211840 | tf_op jit(solution)/shard_map/all_to_all | solution.py:93
  133.9 3.1 %copy-start.5 = (f32[2,30,4608]{2,1,0:T(8,128)S(1)}, f32[2,30,4608]{2,1,0:T(8,128)}, u32[]{:S(2)}) copy-start(f32[2,30,4608]{2,1,0:T(8,128)} %reshape.48) | copy-start | bytes 3317764
  137.1 1.1 copy-start.3
  164.5 37.4 %all-to-all-start.7 = ((bf16[8,2,34560]{2,1,0:T(2,128)(2,1)}), bf16[8,2,34560]{2,1,0:T(2,128)(2,1)}, u32[]{:S(2)}, u32[]{:S(2)}) async-start(bf16[8,2,34560]{2,1,0:T(2,128)(2,1)} %reshape.65), calls=%async_computation.7 | async-start | bytes 2211840 | tf_op jit(solution)/shard_map/all_to_all | solution.py:51
  215.8 66.5 %copy-start.1 = (bf16[480,480]{1,0:T(8,128)(2,1)S(1)}, bf16[480,480]{1,0:T(8,128)(2,1)}, u32[]{:S(2)}) copy-start(bf16[480,480]{1,0:T(8,128)(2,1)} %param.10) | copy-start | bytes 1382404
where the time goes:
time: 284 us; the launch traced here: 282 us
  local copies, waits for them, and re-layouts  122 us (43%)
  blocking collectives  89.6 us (32%)
  starting transfers between devices  33.4 us (12%)
  waiting for transfers between devices  21.3 us (8%)
  matrix products  7.62 us (3%)
  other arithmetic  7.03 us (2%)
    psum x4, blocking collectives, by_axis(): return functools.reduce(lax.psum, axes, array)  63.7 us
    unnamed x32, local copies, waits for them, and re-layouts  59.5 us
    all_to_all x1, blocking collectives, local(): lax.all_to_all(trial_doubles, VIRT, split_axis=2, concat_axis=1, tiled=True)  18.6 us
    all_to_all x2, starting transfers between devices, from_everyone(): return lax.all_to_all(copies, axis, split_axis=0, concat_axis=0, tiled=True)  13.7 us
    all_to_all x1, waiting for transfers between devices, local(): lax.all_to_all(gathered, 'root', split_axis=2, concat_axis=0, tiled=True)  13.1 us
    all_to_all x1, local copies, waits for them, and re-layouts, local(): lax.all_to_all(gathered, 'root', split_axis=2, concat_axis=0, tiled=True)  10.4 us
    reshape x1, local copies, waits for them, and re-layouts, laid_out(): parts.reshape(*shape[:dim], shape[dim] * shape[dim + 1], *shape[dim + 2:])  8.62 us
    all_to_all x1, blocking collectives, sum_at_owner(): lax.all_to_all(parts, axis, split_axis=0, concat_axis=0, tiled=True)  7.36 us
  transfers between devices with their start and end apart: 6, of which 3 were waited for; matrix products, arithmetic and copies ran while one was open for 37% of the time, Pallas kernels for 0%

commit v1 on v0

--- a/solution.py
+++ b/solution.py
@@ -106,7 +106,12 @@
     product = jnp.einsum(
         "ac,ncp->nap",
         virt_fock,
-        lax.all_to_all(trial_doubles, VIRT, split_axis=2, concat_axis=1, tiled=True),
+        jnp.concatenate(
+            lax.all_to_all(
+                jnp.stack(jnp.split(trial_doubles, lax.axis_size(VIRT), 2), 0), VIRT, 0, 0
+            ),
+            1,
+        ),
         preferred_element_type=jnp.float32,
     ).astype(jnp.bfloat16)
     vv_term = lax.all_to_all(product, VIRT, split_axis=1, concat_axis=2, tiled=True)

time: 284 us -> 265 us (0.933)
  local copies, waits for them, and re-layouts: 122 us -> 103 us
    unnamed x32 -> x44, local copies, waits for them, and re-layouts: 59.5 us -> 44 us
    all_to_all x1 -> x0, local copies, waits for them, and re-layouts: 5.49 us -> none  [local(): lax.all_to_all(trial_doubles, VIRT, split_axis=2, concat_axis=1, tiled=True)]
  transfers between devices with their start and end apart: 6 -> 6, of which waited for: 3 -> 3; matrix products, arithmetic and copies ran while one was open for 37% -> 36% of each run, Pallas kernels for 0% -> 0%
where the time goes in v1:
time: 265 us; the launch traced here: 264 us
  local copies, waits for them, and re-layouts  103 us (39%)
  blocking collectives  91 us (34%)
  starting transfers between devices  34.9 us (13%)
  waiting for transfers between devices  18.6 us (7%)
  matrix products  8.63 us (3%)
  other arithmetic  7.03 us (3%)
    psum x4, blocking collectives, by_axis(): return functools.reduce(lax.psum, axes, array)  64.2 us
    unnamed x44, local copies, waits for them, and re-layouts  44 us
    all_to_all x1, blocking collectives, local(): lax.all_to_all(jnp.stack(jnp.split(trial_doubles, lax.axis_size(VIRT), 2)...  17.7 us
    all_to_all x2, starting transfers between devices, from_everyone(): return lax.all_to_all(copies, axis, split_axis=0, concat_axis=0, tiled=True)  15.1 us
    all_to_all x1, waiting for transfers between devices, local(): lax.all_to_all(gathered, 'root', split_axis=2, concat_axis=0, tiled=True)  13.1 us
    all_to_all x1, local copies, waits for them, and re-layouts, local(): lax.all_to_all(gathered, 'root', split_axis=2, concat_axis=0, tiled=True)  10.4 us
    all_to_all x1, blocking collectives, sum_at_owner(): lax.all_to_all(parts, axis, split_axis=0, concat_axis=0, tiled=True)  9.03 us
    reshape x1, local copies, waits for them, and re-layouts, laid_out(): parts.reshape(*shape[:dim], shape[dim] * shape[dim + 1], *shape[dim + 2:])  8.62 us
  transfers between devices with their start and end apart: 6, of which 3 were waited for; matrix products, arithmetic and copies ran while one was open for 36% of the time, Pallas kernels for 0%

profile of v1, /device:TPU:1, one launch (start us, length us, event | category | flops | bytes accessed | tf_op | source)
XLA Modules:
  0.0 263.7 jit_solution(7737383282119343814)
XLA Ops:
  0.6 2.7 %broadcast_in_dim.12 = bf16[2,2,30,4608]{3,1,2,0:T(2,128)(2,1)} broadcast(bf16[2,30,4608]{2,0,1:T(2,128)(2,1)} %param.8), dimensions={1,2,3} | broadcast | bytes 1658880 | tf_op jit(solution)/shard_map/broadcast_in_dim | solution.py:20
  3.3 6.9 %all-to-all-start.5 = ((bf16[2,2,30,4608]{3,1,2,0:T(2,128)(2,1)}), bf16[2,2,30,4608]{3,1,2,0:T(2,128)(2,1)S(1)}, u32[]{:S(2)}, u32[]{:S(2)}) async-start(bf16[2,2,30,4608]{3,1,2,0:T(2,128)(2,1)} %broadcast_in_dim.12), calls=%async_computation.5 | async-start | bytes 2211840 | tf_op jit(solution)/shard_map/all_to_all | solution.py:21
  12.1 17.7 %all_to_all.77 = bf16[16,2,30,288]{3,1,2,0:T(2,128)(2,1)} all-to-all(bf16[16,2,30,288]{3,1,2,0:T(2,128)(2,1)S(1)} %bitcast_dynamic-update-slice_fusion), channel_id=1, replica_groups=mesh['root'=8,'virt_0'=4,'virt_1'=4,'occ'=2] {'virt_0','virt_1'}, dimensions={0} | all-to-all | bytes 1105920 | tf_op jit(solution)/shard_map/all_to_all | solution.py:110
  30.4 8.2 %all-to-all-start.2 = ((bf16[8,2,96]{2,1,0:T(2,128)(2,1)}), bf16[8,2,96]{2,1,0:T(2,128)(2,1)S(1)}, u32[]{:S(2)}, u32[]{:S(2)}) async-start(bf16[8,2,96]{2,1,0:T(2,128)(2,1)} %broadcast_in_dim.11), calls=%async_computation.2 | async-start | bytes 8192 | tf_op jit(solution)/shard_map/all_to_all | solution.py:21
  40.3 1.9 copy.69
  42.2 2.8 %all-to-all-done.2 = bf16[8,2,96]{2,1,0:T(2,128)(2,1)S(1)} async-done(((bf16[8,2,96]{2,1,0:T(2,128)(2,1)}), bf16[8,2,96]{2,1,0:T(2,128)(2,1)S(1)}, u32[]{:S(2)}, u32[]{:S(2)}) %all-to-all-start.2) | async-done | bytes 3104 | tf_op jit(solution)/shard_map/all_to_all | solution.py:21
  45.0 4.3 %all-to-all-start.1 = ((bf16[2,480,288]{2,0,1:T(2,128)(2,1)}), bf16[2,480,288]{2,0,1:T(2,128)(2,1)}, u32[]{:S(2)}, u32[]{:S(2)}) async-start(bf16[2,480,288]{2,0,1:T(2,128)(2,1)} %copy.69), calls=%async_computation.1 | async-start | bytes 1474560 | tf_op jit(solution)/shard_map/all_to_all | solution.py:117
  49.3 3.9 %copy.102 = bf16[30,6,8,1152]{3,2,0,1:T(8,128)(2,1)} copy(bf16[30,6,8,1152]{3,2,1,0:T(8,128)(2,1)} %bitcast.110) | data formatting | bytes 6635520 | tf_op jit(solution)/shard_map/reshape | solution.py:104
  53.2 2.6 fusion
  57.4 2.7 %all-to-all-done.1 = bf16[2,480,288]{2,0,1:T(2,128)(2,1)} async-done(((bf16[2,480,288]{2,0,1:T(2,128)(2,1)}), bf16[2,480,288]{2,0,1:T(2,128)(2,1)}, u32[]{:S(2)}, u32[]{:S(2)}) %all-to-all-start.1) | async-done | bytes 552992 | tf_op jit(solution)/shard_map/all_to_all | solution.py:117
  60.1 4.4 %all-to-all-start.3 = ((bf16[16,30,1152]{2,1,0:T(8,128)(2,1)}), bf16[16,30,1152]{2,1,0:T(8,128)(2,1)}, u32[]{:S(2)}, u32[]{:S(2)}) async-start(bf16[16,30,1152]{2,1,0:T(8,128)(2,1)} %convert_element_type.44), calls=%async_computation.3 | async-start | bytes 2359296 | tf_op jit(solution)/shard_map/all_to_all | solution.py:119
  66.3 8.6 %copy.94 = bf16[2,30,2,4608]{1,0,3,2:T(2,128)(2,1)} copy(bf16[2,30,2,4608]{3,0,1,2:T(2,128)(2,1)S(1)} %bitcast.102) | data formatting | bytes 2211840 | tf_op jit(solution)/shard_map/reshape | solution.py:16
  81.7 10.4 %reshape.69 = bf16[8,2,34560]{2,1,0:T(2,128)(2,1)} reshape(bf16[9216,2,30]{2,1,0:T(2,128)(2,1)} %bitcast.97) | data formatting | bytes 2211840
  95.7 1.9 copy.117
  98.9 9.0 %all_to_all.78 = bf16[2,2,30,4608]{3,1,2,0:T(2,128)(2,1)} all-to-all(bf16[2,2,30,4608]{3,1,2,0:T(2,128)(2,1)S(1)} %copy.73), channel_id=1, replica_groups=mesh['root'=8,'virt_0'=4,'virt_1'=4,'occ'=2] {'occ'}, dimensions={0} | all-to-all | bytes 2211840 | tf_op jit(solution)/shard_map/all_to_all | solution.py:39
  108.0 6.8 %all-to-all-start.6 = ((bf16[8,2,34560]{2,1,0:T(2,128)(2,1)}), bf16[8,2,34560]{2,1,0:T(2,128)(2,1)}, u32[]{:S(2)}, u32[]{:S(2)}) async-start(bf16[8,2,34560]{2,1,0:T(2,128)(2,1)} %reshape.69), calls=%async_computation.6 | async-start | bytes 2211840 | tf_op jit(solution)/shard_map/all_to_all | solution.py:93
  114.7 3.1 %convert_reduce_fusion = f32[2,30,4608]{2,0,1:T(2,128)S(1)} fusion(bf16[2,2,30,4608]{3,1,2,0:T(2,128)(2,1)} %all_to_all.78), kind=kLoop, calls=%fused_computation.2 | loop fusion | flops 829440 | bytes 2211840 | tf_op jit(solution)/shard_map/reduce_sum | solution.py:40
  120.2 5.5 %copy.87 = bf16[2,60,4608]{1,0,2:T(2,128)(2,1)S(1)} copy(bf16[2,60,4608]{2,1,0:T(8,128)(2,1)} %pad_maximum_fusion) | data formatting | bytes 2211840 | tf_op jit(solution)/shard_map/concatenate | solution.py:48
  125.7 6.5 %reshape.71 = bf16[8,2,34560]{2,1,0:T(2,128)(2,1)} reshape(bf16[4608,2,60]{2,1,0:T(2,128)(2,1)S(1)} %bitcast.103) | data formatting | bytes 2211840
  132.2 13.1 %all-to-all-done.6 = bf16[8,2,34560]{2,1,0:T(2,128)(2,1)} async-done(((bf16[8,2,34560]{2,1,0:T(2,128)(2,1)}), bf16[8,2,34560]{2,1,0:T(2,128)(2,1)}, u32[]{:S(2)}, u32[]{:S(2)}) %all-to-all-start.6) | async-done | bytes 1105952 | tf_op jit(solution)/shard_map/all_to_all | solution.py:93
  145.3 4.3 %all-to-all-start.7 = ((bf16[8,2,34560]{2,1,0:T(2,128)(2,1)}), bf16[8,2,34560]{2,1,0:T(2,128)(2,1)}, u32[]{:S(2)}, u32[]{:S(2)}) async-start(bf16[8,2,34560]{2,1,0:T(2,128)(2,1)} %reshape.71), calls=%async_computation.7 | async-start | bytes 2211840 | tf_op jit(solution)/shard_map/all_to_all | solution.py:51
  149.6 3.9 %copy.103 = bf16[30,6,8,1152]{3,2,0,1:T(8,128)(2,1)} copy(bf16[30,6,8,1152]{3,2,1,0:T(8,128)(2,1)} %bitcast.111) | data formatting | bytes 6635520 | tf_op jit(solution)/shard_map/reshape | solution.py:61
  153.5 14.0 %reshape.70 = bf16[9216,2,30]{2,1,0:T(2,128)(2,1)} reshape(bf16[8,2,34560]{2,1,0:T(2,128)(2,1)} %all-to-all-done.6) | data formatting | bytes 2211840
  167.4 10.4 %copy.96 = bf16[2,30,8,1152]{3,1,0,2:T(8,128)(2,1)S(1)} copy(bf16[2,30,8,1152]{1,0,3,2:T(2,128)(2,1)} %bitcast.98) | data formatting | bytes 2211840 | tf_op jit(solution)/shard_map/all_to_all | solution.py:93
  178.2 2.9 %fusion.21 = f32[16,48]{1,0:T(8,128)S(1)} fusion(bf16[16,34560]{1,0:T(8,128)(2,1)S(1)} %bitcast.107, bf16[48,34560]{1,0:T(8,128)(2,1)} %bitcast.99), kind=kOutput, calls=%fused_computation.52 | convolution fusion | flops 53084160 | bytes 4426752 | tf_op jit(solution)/shard_map/dot_general | solution.py:59
  182.7 8.2 %reshape.72 = bf16[4608,2,60]{2,1,0:T(2,128)(2,1)S(1)} reshape(bf16[8,2,34560]{2,1,0:T(2,128)(2,1)} %all-to-all-done.7) | data formatting | bytes 2211840
  190.9 3.4 %copy.97 = bf16[2,60,8,576]{3,2,0,1:T(8,128)(2,1)} copy(bf16[2,60,8,576]{1,0,3,2:T(2,128)(2,1)S(1)} %bitcast.104) | data formatting | bytes 2211840 | tf_op jit(solution)/shard_map/all_to_all | solution.py:51
  194.4 2.3 copy.89
  198.0 22.8 %all-reduce = (f32[16,96]{1,0:T(8,128)S(1)}, f32[16,16]{1,0:T(8,128)S(1)}) all-reduce(f32[16,96]{1,0:T(8,128)S(1)} %dynamic_update_slice.3, f32[16,16]{1,0:T(8,128)S(1)} %convolution_bitcast_fusion.1), channel_id=1, replica_groups=mesh['root'=8,'virt_0'=4,'virt_1'=4,'occ'=2] {'root'}, use_global_device_ids=true, to_apply=%region_1.0 | all-reduce | flops 1792 | bytes 14336 | tf_op jit(solution)/shard_map/psum | solution.py:29
  220.9 11.3 %all-reduce.2 = (f32[16,96]{1,0:T(8,128)S(1)}, f32[16,16]{1,0:T(8,128)S(1)}) all-reduce(f32[16,96]{1,0:T(8,128)S(1)} %get-tuple-element.12, f32[16,16]{1,0:T(8,128)S(1)} %get-tuple-element.13), channel_id=1, replica_groups=mesh['root'=8,'virt_0'=4,'virt_1'=4,'occ'=2] {'virt_0'}, use_global_device_ids=true, to_apply=%region_2.0 | all-reduce | flops 1792 | bytes 14336 | tf_op jit(solution)/shard_map/psum | solution.py:29
  232.2 11.9 %all-reduce.1 = (f32[16,96]{1,0:T(8,128)S(1)}, f32[16,16]{1,0:T(8,128)S(1)}) all-reduce(f32[16,96]{1,0:T(8,128)S(1)} %get-tuple-element.16, f32[16,16]{1,0:T(8,128)S(1)} %get-tuple-element.17), channel_id=1, replica_groups=mesh['root'=8,'virt_0'=4,'virt_1'=4,'occ'=2] {'virt_1'}, use_global_device_ids=true, to_apply=%region_3.0 | all-reduce | flops 1792 | bytes 14336 | tf_op jit(solution)/shard_map/psum | solution.py:29
  244.2 18.1 %all-reduce.3 = (f32[16,96]{1,0:T(8,128)S(1)}, f32[16,16]{1,0:T(8,128)S(1)}) all-reduce(f32[16,96]{1,0:T(8,128)S(1)} %get-tuple-element.14, f32[16,16]{1,0:T(8,128)S(1)} %get-tuple-element.15), channel_id=1, replica_groups=mesh['root'=8,'virt_0'=4,'virt_1'=4,'occ'=2] {'occ'}, use_global_device_ids=true, to_apply=%region_4.0 | all-reduce | flops 1792 | bytes 14336 | tf_op jit(solution)/shard_map/psum | solution.py:29
  (71 shorter events, 26.2 us)
Async XLA Ops:
  0.6 37.9 %copy-start = (bf16[480,480]{1,0:T(8,128)(2,1)S(1)}, bf16[480,480]{1,0:T(8,128)(2,1)}, u32[]{:S(2)}) copy-start(bf16[480,480]{1,0:T(8,128)(2,1)} %param.10) | copy-start | bytes 1382404
  3.3 6.9 %copy-start.2 = (bf16[2,30,4608]{2,0,1:T(2,128)(2,1)S(1)}, bf16[2,30,4608]{2,0,1:T(2,128)(2,1)}, u32[]{:S(2)}) copy-start(bf16[2,30,4608]{2,0,1:T(2,128)(2,1)} %param.8) | copy-start | bytes 1658884
  3.3 8.7 %all-to-all-start.5 = ((bf16[2,2,30,4608]{3,1,2,0:T(2,128)(2,1)}), bf16[2,2,30,4608]{3,1,2,0:T(2,128)(2,1)S(1)}, u32[]{:S(2)}, u32[]{:S(2)}) async-start(bf16[2,2,30,4608]{3,1,2,0:T(2,128)(2,1)} %broadcast_in_dim.12), calls=%async_computation.5 | async-start | bytes 2211840 | tf_op jit(solution)/shard_map/all_to_all | solution.py:21
  10.9 18.9 %copy-start.9 = (bf16[2,96]{1,0:T(2,128)(2,1)S(1)}, bf16[2,96]{1,0:T(2,128)(2,1)}, u32[]{:S(2)}) copy-start(bf16[2,96]{1,0:T(2,128)(2,1)} %param.7) | copy-start | bytes 1156
  30.4 14.7 %all-to-all-start.2 = ((bf16[8,2,96]{2,1,0:T(2,128)(2,1)}), bf16[8,2,96]{2,1,0:T(2,128)(2,1)S(1)}, u32[]{:S(2)}, u32[]{:S(2)}) async-start(bf16[8,2,96]{2,1,0:T(2,128)(2,1)} %broadcast_in_dim.11), calls=%async_computation.2 | async-start | bytes 8192 | tf_op jit(solution)/shard_map/all_to_all | solution.py:21
  45.0 15.0 %all-to-all-start.1 = ((bf16[2,480,288]{2,0,1:T(2,128)(2,1)}), bf16[2,480,288]{2,0,1:T(2,128)(2,1)}, u32[]{:S(2)}, u32[]{:S(2)}) async-start(bf16[2,480,288]{2,0,1:T(2,128)(2,1)} %copy.69), calls=%async_computation.1 | async-start | bytes 1474560 | tf_op jit(solution)/shard_map/all_to_all | solution.py:117
  60.1 35.6 %all-to-all-start.3 = ((bf16[16,30,1152]{2,1,0:T(8,128)(2,1)}), bf16[16,30,1152]{2,1,0:T(8,128)(2,1)}, u32[]{:S(2)}, u32[]{:S(2)}) async-start(bf16[16,30,1152]{2,1,0:T(8,128)(2,1)} %convert_element_type.44), calls=%async_computation.3 | async-start | bytes 2359296 | tf_op jit(solution)/shard_map/all_to_all | solution.py:119
  74.9 1.6 copy-start.8
  77.0 1.8 copy-start.3
  81.7 10.4 %copy-start.10 = (s32[16]{0:T(128)S(1)}, s32[16]{0:T(128)}, u32[]{:S(2)}) copy-start(s32[16]{0:T(128)} %param.13) | copy-start | bytes 196
  107.9 9.9 %copy-start.6 = (f32[2,30,4608]{2,1,0:T(8,128)S(1)}, f32[2,30,4608]{2,1,0:T(8,128)}, u32[]{:S(2)}) copy-start(f32[2,30,4608]{2,1,0:T(8,128)} %reshape.58) | copy-start | bytes 3317764
  107.9 9.9 %copy-start.7 = (f32[2,30,4608]{2,1,0:T(8,128)S(1)}, f32[2,30,4608]{2,1,0:T(8,128)}, u32[]{:S(2)}) copy-start(f32[2,30,4608]{2,1,0:T(8,128)} %reshape.68) | copy-start | bytes 3317764
  108.0 37.4 %all-to-all-start.6 = ((bf16[8,2,34560]{2,1,0:T(2,128)(2,1)}), bf16[8,2,34560]{2,1,0:T(2,128)(2,1)}, u32[]{:S(2)}, u32[]{:S(2)}) async-start(bf16[8,2,34560]{2,1,0:T(2,128)(2,1)} %reshape.69), calls=%async_computation.6 | async-start | bytes 2211840 | tf_op jit(solution)/shard_map/all_to_all | solution.py:93
  114.7 3.1 %copy-start.5 = (f32[2,30,4608]{2,1,0:T(8,128)S(1)}, f32[2,30,4608]{2,1,0:T(8,128)}, u32[]{:S(2)}) copy-start(f32[2,30,4608]{2,1,0:T(8,128)} %reshape.56) | copy-start | bytes 3317764
  117.9 1.1 copy-start.4
  145.3 37.4 %all-to-all-start.7 = ((bf16[8,2,34560]{2,1,0:T(2,128)(2,1)}), bf16[8,2,34560]{2,1,0:T(2,128)(2,1)}, u32[]{:S(2)}, u32[]{:S(2)}) async-start(bf16[8,2,34560]{2,1,0:T(2,128)(2,1)} %reshape.71), calls=%async_computation.7 | async-start | bytes 2211840 | tf_op jit(solution)/shard_map/all_to_all | solution.py:51
  196.6 67.0 %copy-start.1 = (bf16[480,480]{1,0:T(8,128)(2,1)S(1)}, bf16[480,480]{1,0:T(8,128)(2,1)}, u32[]{:S(2)}) copy-start(bf16[480,480]{1,0:T(8,128)(2,1)} %param.10) | copy-start | bytes 1382404
